TPU v7x, 256 devices: a 2x2x32 block of a 4x8x32 slice. The times are simulated.
256 devices in a mesh: beam: 4 (over x, y), tm: 32 (over z), sub: 2 (over core).
Axes of the slice: x: 2, y: 2, z: 32, core: 2. Of those that a mesh axis runs over, the one named last changes fastest.
The devices are a block of a 4x8x32 slice.
Arguments:
- channels: bfloat16 [2, 8192, 4096], P(None, ('beam', 'tm'), 'sub'), parts along dimension 1, may hold values from -6 to 6
- synth_taps: float32 [4, 2, 2048], P(None, 'sub'), may hold values from 0.2 to 1
- chirp_phase: float32 [2048, 4096], P('tm', 'sub'), may hold values from -3.140625 to 3.140625
Outputs:
- dedispersed: float32 [2, 8192, 2, 2048], P(None, ('beam', 'tm'), 'sub'), parts along dimension 1
There are 4 independent parts, one for each index of `beam`. A program takes and returns all parts, laid end to end along the dimension named above; an argument that names none is the same for every part. Nothing has to cross between parts.
All inputs are finite; a program needn't handle non-finite values.
Results may differ from a plain program's by a relative error of at most 0.0003.
Values may be sent and summed in bfloat16 or wider, within the bound.
A program may use at most 64 MiB of HBM per device.

v0:
```python
import math

import jax
import jax.numpy as jnp
from jax import lax
from jax.sharding import PartitionSpec as P

highest = lax.Precision.HIGHEST
inv_root2 = 1.0 / math.sqrt(2.0)


def partner(x, axis, distance):
    return lax.ppermute(x, axis, [(i, i ^ 1 << distance) for i in range(lax.axis_size(axis))])


def shifted(block, axis, distance):
    devices = range(lax.axis_size(axis))
    route = [(i - distance, i) for i in devices if i - distance in devices]
    return lax.ppermute(block, axis, route)


def roots_table(row_count, col_count, length, direction):
    product = (
        jnp.arange(row_count, dtype=jnp.int32)[:, None]
        * jnp.arange(col_count, dtype=jnp.int32)[None, :]
        % length
    )
    angles = direction * 2.0 * math.pi / length * product.astype(jnp.float32)
    return (jnp.cos(angles), jnp.sin(angles))


def global_roots(left_index, right_index, length, direction):
    product = left_index * right_index % length
    angles = direction * 2.0 * math.pi / length * product.astype(jnp.float32)
    return (jnp.cos(angles), jnp.sin(angles))


def parity_roots(parity_f, half, direction):
    angles = direction * math.pi / half * parity_f * jnp.arange(half, dtype=jnp.float32)
    return (jnp.cos(angles), jnp.sin(angles))


def complex_times(left_re, left_im, right_re, right_im):
    return (left_re * right_re - left_im * right_im, left_re * right_im + left_im * right_re)


def complex_einsum(form, left_re, left_im, right_re, right_im):

    def contract(former, latter):
        return jnp.einsum(form, former, latter, precision=highest)

    return (
        contract(left_re, right_re) - contract(left_im, right_im),
        contract(left_re, right_im) + contract(left_im, right_re),
    )


def dft_last(re_part, im_part, direction):
    length = re_part.shape[-1]
    outer_len = math.gcd(length, 32)
    inner_len = length // outer_len
    leading = re_part.shape[:-1]
    re_part = re_part.reshape(leading + (outer_len, inner_len))
    im_part = im_part.reshape(leading + (outer_len, inner_len))
    table_re, table_im = roots_table(outer_len, outer_len, outer_len, direction)
    re_part, im_part = complex_einsum("...uw,ur->...rw", re_part, im_part, table_re, table_im)
    twist_re, twist_im = roots_table(outer_len, inner_len, length, direction)
    re_part, im_part = complex_times(re_part, im_part, twist_re, twist_im)
    table_re, table_im = roots_table(inner_len, inner_len, inner_len, direction)
    re_part, im_part = complex_einsum("...rw,wt->...tr", re_part, im_part, table_re, table_im)
    factor = 1.0 / math.sqrt(length)
    return (
        re_part.reshape(leading + (length,)) * factor,
        im_part.reshape(leading + (length,)) * factor,
    )


def half_swap(re_part, im_part, sign_own):
    other_re, other_im = partner((re_part, im_part), "sub", 0)
    return (
        (other_re + sign_own * re_part) * inv_root2,
        (other_im + sign_own * im_part) * inv_root2,
    )


def to_columns(re_part, im_part):
    time_count = lax.axis_size("tm")
    time_index = lax.axis_index("tm")
    parity = lax.axis_index("sub")
    half = re_part.shape[1]
    got_re, got_im = (
        lax.all_to_all(re_part.T, "tm", split_axis=0, concat_axis=1, tiled=True),
        lax.all_to_all(im_part.T, "tm", split_axis=0, concat_axis=1, tiled=True),
    )
    col_width = half // time_count
    sample_index = 2 * (time_index * col_width + jnp.arange(col_width, dtype=jnp.int32)) + parity
    return (got_re, got_im, sample_index)


def to_rows(re_part, im_part):
    got_re, got_im = (
        lax.all_to_all(re_part, "tm", split_axis=1, concat_axis=0, tiled=True),
        lax.all_to_all(im_part, "tm", split_axis=1, concat_axis=0, tiled=True),
    )
    return (got_re.T, got_im.T)


def body(channels, synth_taps, chirp_phase):
    frames_dev = channels.shape[1]
    half = channels.shape[2]
    tap_count = synth_taps.shape[0]
    time_index = lax.axis_index("tm")
    time_count = lax.axis_size("tm")
    parity = lax.axis_index("sub")
    parity_f = parity.astype(jnp.float32)
    sign_own = 1.0 - 2.0 * parity_f
    total_frames = frames_dev * time_count
    series_len = total_frames * 2 * half
    partner_re, partner_im = partner((channels[0], channels[1]), "sub", 0)
    mixed_re = (
        partner_re.astype(jnp.float32) + sign_own * channels[0].astype(jnp.float32)
    ) * inv_root2
    mixed_im = (
        partner_im.astype(jnp.float32) + sign_own * channels[1].astype(jnp.float32)
    ) * inv_root2
    turn_re, turn_im = parity_roots(parity_f, half, 1.0)
    mixed_re, mixed_im = complex_times(mixed_re, mixed_im, turn_re, turn_im)
    volt_re, volt_im = dft_last(mixed_re, mixed_im, 1.0)
    keep_from = frames_dev - tap_count + 1
    tail_re, tail_im = shifted((volt_re[keep_from:], volt_im[keep_from:]), "tm", 1)
    long_re = jnp.concatenate([tail_re, volt_re], axis=0)
    long_im = jnp.concatenate([tail_im, volt_im], axis=0)
    synth_re = jnp.zeros_like(volt_re)
    synth_im = jnp.zeros_like(volt_im)
    for offset in range(tap_count):
        begin = tap_count - 1 - offset
        synth_re = synth_re + synth_taps[offset, 0] * long_re[begin : begin + frames_dev]
        synth_im = synth_im + synth_taps[offset, 0] * long_im[begin : begin + frames_dev]
    col_re, col_im, sample_index = to_columns(synth_re, synth_im)
    col_re, col_im = dft_last(col_re, col_im, -1.0)
    bin_index = jnp.arange(total_frames, dtype=jnp.int32)
    twist_re, twist_im = global_roots(sample_index[:, None], bin_index[None, :], series_len, -1.0)
    col_re, col_im = complex_times(col_re, col_im, twist_re, twist_im)
    row_re, row_im = to_rows(col_re, col_im)
    row_re, row_im = dft_last(row_re, row_im, -1.0)
    turn_re, turn_im = parity_roots(parity_f, half, -1.0)
    row_re, row_im = complex_times(row_re, row_im, turn_re, turn_im)
    row_re, row_im = half_swap(row_re, row_im, sign_own)
    row_re, row_im = complex_times(row_re, row_im, jnp.cos(chirp_phase), jnp.sin(chirp_phase))
    row_re, row_im = half_swap(row_re, row_im, sign_own)
    turn_re, turn_im = parity_roots(parity_f, half, 1.0)
    row_re, row_im = complex_times(row_re, row_im, turn_re, turn_im)
    row_re, row_im = dft_last(row_re, row_im, 1.0)
    own_bins = time_index * frames_dev + jnp.arange(frames_dev, dtype=jnp.int32)
    own_samples = 2 * jnp.arange(half, dtype=jnp.int32) + parity
    twist_re, twist_im = global_roots(own_bins[:, None], own_samples[None, :], series_len, 1.0)
    row_re, row_im = complex_times(row_re, row_im, twist_re, twist_im)
    col_re, col_im, ignored = to_columns(row_re, row_im)
    col_re, col_im = dft_last(col_re, col_im, 1.0)
    out_re, out_im = to_rows(col_re, col_im)
    return jnp.stack([out_re, out_im])[:, :, None, :]


def solution(mesh):
    placed = (P(None, ("beam", "tm"), "sub"), P(None, "sub", None), P("tm", "sub"))
    return jax.shard_map(
        body,
        mesh=mesh,
        in_specs=placed,
        out_specs=P(None, ("beam", "tm"), "sub", None),
        check_vma=False,
    )
```

profile of v0, /device:TPU:46, one launch (start us, length us, event | category | flops | bytes accessed | tf_op | source)
XLA Modules:
  0.0 739.9 jit_solution(18036711721346306883)
XLA Ops:
  13.5 4.5 fusion.80
  25.3 4.1 collective-permute-start.2
  29.3 4.7 fusion.14
  38.6 4.1 collective-permute-start.3
  45.6 8.5 %fusion.23 = (f32[64,2048]{0,1:T(8,128)}, f32[64,2048]{0,1:T(8,128)}) fusion(f32[64,2048]{0,1:T(8,128)} %copy-done, f32[3,2048]{0,1:T(8,128)} %copy.212, f32[64,64,32]{0,2,1:T(8,128)S(1)} %copy.210, f32[2048]{0:T(1024)S(1)} %bitcast.308, f32[2048]{0:T(1024)S(1)} %bitcast.309, f32[2048]{0:T(1024)S(1)} %bitcast.307, f32[2048]{0:T(1024)S(1)} %bitcast.306, ...), kind=kLoop, calls=%fused_computation.54 | loop fusion | flops 2621440 | bytes 3227648 | tf_op jit(solution)/shard_map/add | solution.py:138
  56.9 33.2 %all-to-all-start = ((f32[32,1,4096]{2,1,0:T(1,128)}), f32[32,1,4096]{2,1,0:T(1,128)S(1)}, u32[]{:S(2)}, u32[]{:S(2)}) async-start(f32[32,1,4096]{2,1,0:T(1,128)} %reshape.218), calls=%async_computation | async-start | bytes 1048576 | tf_op jit(solution)/shard_map/all_to_all | solution.py:92
  91.6 61.8 %all-to-all-done = f32[32,1,4096]{2,1,0:T(1,128)S(1)} async-done(((f32[32,1,4096]{2,1,0:T(1,128)}), f32[32,1,4096]{2,1,0:T(1,128)S(1)}, u32[]{:S(2)}, u32[]{:S(2)}) %all-to-all-start) | async-done | bytes 524320 | tf_op jit(solution)/shard_map/all_to_all | solution.py:92
  153.4 5.6 all-to-all-start.1
  165.1 55.6 %all-to-all-done.1 = f32[32,1,4096]{2,1,0:T(1,128)} async-done(((f32[32,1,4096]{2,1,0:T(1,128)}), f32[32,1,4096]{2,1,0:T(1,128)}, u32[]{:S(2)}, u32[]{:S(2)}) %all-to-all-start.1) | async-done | bytes 524320 | tf_op jit(solution)/shard_map/all_to_all | solution.py:93
  229.3 4.0 fusion.72
  245.1 4.7 fusion.39
  251.2 5.0 all-to-all-start.2
  257.6 60.2 %all-to-all-done.2 = f32[32,1,4096]{2,1,0:T(1,128)S(1)} async-done(((f32[32,1,4096]{2,1,0:T(1,128)}), f32[32,1,4096]{2,1,0:T(1,128)S(1)}, u32[]{:S(2)}, u32[]{:S(2)}) %all-to-all-start.2) | async-done | bytes 524320 | tf_op jit(solution)/shard_map/all_to_all | solution.py:102
  317.8 4.8 all-to-all-start.3
  329.5 55.1 %all-to-all-done.3 = f32[32,1,4096]{2,1,0:T(1,128)S(1)} async-done(((f32[32,1,4096]{2,1,0:T(1,128)}), f32[32,1,4096]{2,1,0:T(1,128)S(1)}, u32[]{:S(2)}, u32[]{:S(2)}) %all-to-all-start.3) | async-done | bytes 524320 | tf_op jit(solution)/shard_map/all_to_all | solution.py:103
  439.6 5.1 fusion.37
  446.2 4.8 all-to-all-start.4
  452.5 63.6 %all-to-all-done.4 = f32[32,1,4096]{2,1,0:T(1,128)S(1)} async-done(((f32[32,1,4096]{2,1,0:T(1,128)}), f32[32,1,4096]{2,1,0:T(1,128)S(1)}, u32[]{:S(2)}, u32[]{:S(2)}) %all-to-all-start.4) | async-done | bytes 524320 | tf_op jit(solution)/shard_map/all_to_all | solution.py:92
  516.1 5.2 all-to-all-start.5
  527.7 57.3 %all-to-all-done.5 = f32[32,1,4096]{2,1,0:T(1,128)S(1)} async-done(((f32[32,1,4096]{2,1,0:T(1,128)}), f32[32,1,4096]{2,1,0:T(1,128)S(1)}, u32[]{:S(2)}, u32[]{:S(2)}) %all-to-all-start.5) | async-done | bytes 524320 | tf_op jit(solution)/shard_map/all_to_all | solution.py:93
  600.1 4.8 all-to-all-start.6
  614.1 53.4 %all-to-all-done.6 = f32[32,1,4096]{2,1,0:T(1,128)S(1)} async-done(((f32[32,1,4096]{2,1,0:T(1,128)}), f32[32,1,4096]{2,1,0:T(1,128)S(1)}, u32[]{:S(2)}, u32[]{:S(2)}) %all-to-all-start.6) | async-done | bytes 524320 | tf_op jit(solution)/shard_map/all_to_all | solution.py:102
  667.4 5.0 all-to-all-start.7
  675.7 58.5 %all-to-all-done.7 = f32[32,1,4096]{2,1,0:T(1,128)S(1)} async-done(((f32[32,1,4096]{2,1,0:T(1,128)}), f32[32,1,4096]{2,1,0:T(1,128)S(1)}, u32[]{:S(2)}, u32[]{:S(2)}) %all-to-all-start.7) | async-done | bytes 524320 | tf_op jit(solution)/shard_map/all_to_all | solution.py:103
  (150 shorter events, 165.5 us)
Async XLA Ops:
  0.0 3.2 copy-start.5
  1.1 1.7 collective-permute-start
  1.3 1.9 collective-permute-start.1
  7.4 1.2 copy-start.3
  25.3 17.5 %collective-permute-start.2 = (f32[3,2048]{1,0:T(4,128)S(1)}, f32[3,2048]{1,0:T(4,128)S(1)}, u32[]{:S(2)}, u32[]{:S(2)}) collective-permute-start(f32[3,2048]{1,0:T(4,128)S(1)} %copy.203), channel_id=1, source_target_pairs={{0,2},{2,4},{4,6},{6,8},{8,10},{10,12},{12,14},{14,16},{16,18},{18... | collective-permute-start | bytes 73736 | tf_op jit(solution)/shard_map/ppermute | solution.py:19
  37.1 5.6 copy-start.8
  38.6 5.6 collective-permute-start.3
  54.2 36.0 %copy-start.4 = (f32[64,2048]{0,1:T(8,128)S(1)}, f32[64,2048]{0,1:T(8,128)}, u32[]{:S(2)}) copy-start(f32[64,2048]{0,1:T(8,128)} %get-tuple-element.31) | copy-start | bytes 1572868
  56.9 96.4 %all-to-all-start = ((f32[32,1,4096]{2,1,0:T(1,128)}), f32[32,1,4096]{2,1,0:T(1,128)S(1)}, u32[]{:S(2)}, u32[]{:S(2)}) async-start(f32[32,1,4096]{2,1,0:T(1,128)} %reshape.218), calls=%async_computation | async-start | bytes 1048576 | tf_op jit(solution)/shard_map/all_to_all | solution.py:92
  153.4 67.4 %all-to-all-start.1 = ((f32[32,1,4096]{2,1,0:T(1,128)}), f32[32,1,4096]{2,1,0:T(1,128)}, u32[]{:S(2)}, u32[]{:S(2)}) async-start(f32[32,1,4096]{2,1,0:T(1,128)} %reshape.220), calls=%async_computation.1 | async-start | bytes 1048576 | tf_op jit(solution)/shard_map/all_to_all | solution.py:93
  251.2 66.6 %all-to-all-start.2 = ((f32[32,1,4096]{2,1,0:T(1,128)}), f32[32,1,4096]{2,1,0:T(1,128)S(1)}, u32[]{:S(2)}, u32[]{:S(2)}) async-start(f32[32,1,4096]{2,1,0:T(1,128)} %reshape.222), calls=%async_computation.2 | async-start | bytes 1048576 | tf_op jit(solution)/shard_map/all_to_all | solution.py:102
  317.8 66.8 %all-to-all-start.3 = ((f32[32,1,4096]{2,1,0:T(1,128)}), f32[32,1,4096]{2,1,0:T(1,128)S(1)}, u32[]{:S(2)}, u32[]{:S(2)}) async-start(f32[32,1,4096]{2,1,0:T(1,128)} %reshape.224), calls=%async_computation.3 | async-start | bytes 1048576 | tf_op jit(solution)/shard_map/all_to_all | solution.py:103
  388.7 1.6 copy-start.1
  409.6 1.0 copy-start.6
  410.6 1.0 copy-start.7
  410.7 2.7 collective-permute-start.4
  410.9 2.6 collective-permute-start.5
  413.8 2.0 collective-permute-start.6
  414.1 2.5 collective-permute-start.7
  446.2 69.9 %all-to-all-start.4 = ((f32[32,1,4096]{2,1,0:T(1,128)}), f32[32,1,4096]{2,1,0:T(1,128)S(1)}, u32[]{:S(2)}, u32[]{:S(2)}) async-start(f32[32,1,4096]{2,1,0:T(1,128)} %reshape.226), calls=%async_computation.4 | async-start | bytes 1048576 | tf_op jit(solution)/shard_map/all_to_all | solution.py:92
  516.1 68.9 %all-to-all-start.5 = ((f32[32,1,4096]{2,1,0:T(1,128)}), f32[32,1,4096]{2,1,0:T(1,128)S(1)}, u32[]{:S(2)}, u32[]{:S(2)}) async-start(f32[32,1,4096]{2,1,0:T(1,128)} %reshape.228), calls=%async_computation.5 | async-start | bytes 1048576 | tf_op jit(solution)/shard_map/all_to_all | solution.py:93
  587.2 1.6 copy-start.2
  600.1 67.4 %all-to-all-start.6 = ((f32[32,1,4096]{2,1,0:T(1,128)}), f32[32,1,4096]{2,1,0:T(1,128)S(1)}, u32[]{:S(2)}, u32[]{:S(2)}) async-start(f32[32,1,4096]{2,1,0:T(1,128)} %reshape.232), calls=%async_computation.6 | async-start | bytes 1048576 | tf_op jit(solution)/shard_map/all_to_all | solution.py:102
  667.4 66.8 %all-to-all-start.7 = ((f32[32,1,4096]{2,1,0:T(1,128)}), f32[32,1,4096]{2,1,0:T(1,128)S(1)}, u32[]{:S(2)}, u32[]{:S(2)}) async-start(f32[32,1,4096]{2,1,0:T(1,128)} %reshape.230), calls=%async_computation.7 | async-start | bytes 1048576 | tf_op jit(solution)/shard_map/all_to_all | solution.py:103
  (1 other events, 1.0 us)
where the time goes:
time: 751 us; the launch traced here: 740 us
  waiting for transfers between devices  469 us (62%)
  matrix products  104 us (14%)
  starting transfers between devices  78.6 us (10%)
  local copies, waits for them, and re-layouts  50.5 us (7%)
  other arithmetic  36.8 us (5%)
    all_to_all x2, waiting for transfers between devices, to_columns(): lax.all_to_all(re_part.T, 'tm', split_axis=0, concat_axis=1, tiled=True)  125 us
    all_to_all x2, waiting for transfers between devices, to_rows(): lax.all_to_all(im_part, 'tm', split_axis=1, concat_axis=0, tiled=True)  114 us
    all_to_all x2, waiting for transfers between devices, to_rows(): lax.all_to_all(re_part, 'tm', split_axis=1, concat_axis=0, tiled=True)  114 us
    all_to_all x2, waiting for transfers between devices, to_columns(): lax.all_to_all(im_part.T, 'tm', split_axis=0, concat_axis=1, tiled=True)  113 us
    dot_general x40, matrix products, contract(): return jnp.einsum(form, former, latter, precision=highest)  104 us
    all_to_all x2, starting transfers between devices, to_columns(): lax.all_to_all(re_part.T, 'tm', split_axis=0, concat_axis=1, tiled=True)  38 us
    unnamed x36, local copies, waits for them, and re-layouts  19.3 us
  transfers between devices with their start and end apart: 16, of which 13 were waited for; matrix products, arithmetic and copies ran while one was open for 6% of the time, Pallas kernels for 0%

commit v1 on v0

v1 whole, which is shorter than its diff:
```python
import functools
import math

import jax
import jax.numpy as jnp
import numpy as np
from jax import lax
from jax.experimental import pallas as pl
from jax.experimental.pallas import tpu as pltpu
from jax.sharding import PartitionSpec as P

MESH = pl.DeviceIdType.MESH
f32 = jnp.float32
bf16 = jnp.bfloat16

WIDTH = 64
LANES = 2 * WIDTH
SUB = 8

SPAN = 160.0
BASE = SPAN / 2
FLOOR = 1e-35


def halves():
    lane = lax.broadcasted_iota(jnp.int32, (1, LANES), 1)
    return jnp.where(lane < WIDTH, -1.0, 1.0).astype(f32)


def swap(x):
    return pltpu.roll(x, WIDTH, x.ndim - 1)


def turned(x, table, conj=False):
    re, im = table
    return x * re - swap(x) * im if conj else x * re + swap(x) * im


def split(x):
    hi = x.astype(bf16)
    return hi, (x - hi.astype(f32)).astype(bf16)


def dot(a, b):
    return lax.dot_general(a, b, (((1,), (0,)), ((), ())), preferred_element_type=f32)


def left(matrix, blocks, conj):
    hi_ref, lo_ref = matrix
    sign = -halves() if conj else halves()
    tall = [jnp.concatenate([x, swap(x) * sign], axis=0) for x in blocks]
    hi, lo = split(jnp.concatenate(tall, axis=1))
    w_hi, w_lo = hi_ref[...], lo_ref[...]
    out = dot(w_hi, hi) + (dot(w_hi, lo) + dot(w_lo, hi))
    return [out[:, i * LANES : (i + 1) * LANES] for i in range(len(blocks))]


def right(matrix, x):
    hi_ref, lo_ref = matrix
    hi, lo = split(x)
    w_hi, w_lo = hi_ref[...], lo_ref[...]
    return dot(hi, w_hi) + (dot(lo, w_hi) + dot(hi, w_lo))


def encode(x, norm):
    top = jnp.maximum(jnp.max(jnp.abs(x), axis=0, keepdims=True), FLOOR)
    size = jnp.exp(jnp.abs(x) * (SPAN / top) - BASE)
    return jnp.where(x < 0, -size, size).astype(bf16), top * (norm / SPAN)


def decode(code, scale):
    code = code.astype(f32)
    size = jnp.log(jnp.abs(code)) + BASE
    return jnp.where(code < 0, -size, size) * scale


def circle(x):
    turns = jnp.floor(4.0 * x + 0.5)
    y = (2.0 * math.pi) * (x - 0.25 * turns)
    y2 = y * y
    sin = y * (1.0 + y2 * (-1.0 / 6 + y2 * (1.0 / 120 + y2 * (-1.0 / 5040 + y2 * (1.0 / 362880)))))
    cos = 1.0 + y2 * (-0.5 + y2 * (1.0 / 24 + y2 * (-1.0 / 720 + y2 * (1.0 / 40320))))
    quarter = turns - 4.0 * jnp.floor(0.25 * turns)
    odd = (quarter == 1.0) | (quarter == 3.0)
    flip_cos = (quarter == 1.0) | (quarter == 2.0)
    flip_sin = quarter >= 2.0
    first, second = jnp.where(odd, sin, cos), jnp.where(odd, cos, sin)
    return jnp.where(flip_cos, -first, first), jnp.where(flip_sin, -second, second)


def route(i, n):
    return n // 2 + (i + 1) // 2 * (2 * lax.rem(i, 2) - 1)


def beam_kernel(norm_in, norm_out, own, other, taps, phase_ref, turns_re, turns_im, twist_re, twist_im, long_hi, long_lo,
                inner_hi, inner_lo, outer_hi, outer_lo, plus_hi, plus_lo, minus_hi, minus_lo, out_ref, x_ref, v_ref, u_ref,
                z_ref, line_ref, t1_re, t1_im, t2_re, t2_im, resp_re, resp_im, mine_ref, theirs_ref, put, put_scale, got,
                got_scale, sent, arrived, sent_scale, arrived_scale, half_sent, half_arrived):
    n, rows, _ = x_ref.shape
    radix, length, _ = u_ref.shape
    step = length // radix
    chunks = rows // (2 * SUB)
    me = lax.axis_index("tm")
    parity = lax.axis_index("sub")
    long_m, inner_m, outer_m = (long_hi, long_lo), (inner_hi, inner_lo), (outer_hi, outer_lo)
    plus_m, minus_m = (plus_hi, plus_lo), (minus_hi, minus_lo)
    turn_re, turn_im = turns_re.at[parity], turns_im.at[parity]
    sign = 1.0 - 2.0 * parity.astype(f32)

    barrier = pltpu.get_barrier_semaphore()

    def greet(i, carry):
        peer = lax.rem(me + route(i, n), n)
        pl.semaphore_signal(barrier, inc=1, device_id={"tm": peer}, device_id_type=MESH)
        return carry

    lax.fori_loop(0, n - 1, greet, 0)
    pl.semaphore_signal(barrier, inc=1, device_id={"sub": 1 - parity}, device_id_type=MESH)

    def copies(phase, i, peer, slot):
        pairs = ((put_scale, got_scale, sent_scale, arrived_scale), (put, got, sent, arrived))
        return [
            pltpu.make_async_remote_copy(
                src_ref=source.at[phase, peer],
                dst_ref=target.at[phase, slot],
                send_sem=out_sem.at[phase, i],
                recv_sem=in_sem.at[phase, i],
                device_id={"tm": peer},
                device_id_type=MESH,
            )
            for source, target, out_sem, in_sem in pairs
        ]

    def send_all(phase, held, norm):

        def send(i, carry):
            peer = lax.rem(me + route(i, n), n)
            put[phase, peer], put_scale[phase, peer] = encode(held(peer), norm)
            for copy in copies(phase, i, peer, me):
                copy.start()
            return carry

        lax.fori_loop(0, n - 1, send, 0)
        got[phase, me], got_scale[phase, me] = encode(held(me), norm)

    def receive_all(phase, use):
        use(me, decode(got[phase, me], got_scale[phase, me]))

        def receive(i, carry):
            d = route(i, n)
            source = lax.rem(me + n - d, n)
            for copy in copies(phase, i, lax.rem(me + d, n), source):
                copy.wait_recv()
            use(source, decode(got[phase, source], got_scale[phase, source]))
            return carry

        lax.fori_loop(0, n - 1, receive, 0)

    def pair_of(c):
        return [pl.ds(pl.multiple_of((2 * c + i) * SUB, SUB), SUB) for i in range(2)]

    def across(c, blocks, conj):
        return [y.reshape(n, SUB, LANES) for y in left(long_m, [x.reshape(n * SUB, LANES) for x in blocks], conj)]

    def row_out(t):
        return right(plus_m, turned(v_ref[t], (twist_re[t], twist_im[t])))

    low = lax.broadcasted_iota(jnp.int32, (1, LANES), 1) < WIDTH
    for j in range(n // 2):
        cols = slice(j * LANES, (j + 1) * LANES)
        re = other[0, :, cols].astype(f32) + sign * own[0, :, cols].astype(f32)
        im = other[1, :, cols].astype(f32) + sign * own[1, :, cols].astype(f32)
        even = jnp.where(low, re, swap(im))
        odd = jnp.where(low, swap(re), im)
        x_ref[2 * j] = turned(even, (turn_re[2 * j], turn_im[2 * j]))
        x_ref[2 * j + 1] = turned(odd, (turn_re[2 * j + 1], turn_im[2 * j + 1]))

    def first_rows(c, carry):
        parts = pair_of(c)
        for part, y in zip(parts, across(c, [x_ref[:, part, :] for part in parts], True)):
            v_ref[:, part, :] = y
        return carry

    lax.fori_loop(0, chunks, first_rows, 0)
    pl.semaphore_wait(barrier, n)
    send_all(0, row_out, norm_in)

    lane = lax.broadcasted_iota(jnp.int32, (1, LANES), 1)
    row = lax.broadcasted_iota(jnp.int32, (length, 1), 0)
    column = 2 * (n * lax.rem(lane, WIDTH) + me) + parity
    frames = radix * length
    series_len = frames * 2 * WIDTH * n

    def column_tables(q, carry):
        cos, sin = circle((q * row).astype(f32) * (-1.0 / frames) + jnp.zeros((1, LANES), f32))
        t1_re[q], t1_im[q] = cos, sin * halves()
        cos, sin = circle(((q + radix * row) * column).astype(f32) * (-1.0 / series_len))
        t2_re[q], t2_im[q] = cos, sin * halves()
        return carry

    lax.fori_loop(0, radix, column_tables, 0)

    for j in range(n // 2):
        cos, sin = circle(phase_ref[:, j * LANES : (j + 1) * LANES] * (0.5 / math.pi))
        line_ref[2 * j * rows : (2 * j + 1) * rows] = cos
        line_ref[(2 * j + 1) * rows : (2 * j + 2) * rows] = sin
    for j in range(n // 2):
        for q in range(radix):
            part = slice(q * SUB, (q + 1) * SUB)
            cos = line_ref[pl.ds(2 * j * rows + q, SUB, stride=rows // SUB)]
            sin = line_ref[pl.ds((2 * j + 1) * rows + q, SUB, stride=rows // SUB)]
            far_cos, far_sin = swap(cos), swap(sin)
            resp_re[2 * j, part], resp_im[2 * j, part] = jnp.where(low, cos, far_cos), jnp.where(low, -sin, far_sin)
            resp_re[2 * j + 1, part] = jnp.where(low, far_cos, cos)
            resp_im[2 * j + 1, part] = jnp.where(low, -far_sin, sin)

    line_ref[0:SUB] = jnp.zeros((SUB, LANES), f32)

    def to_line(t, x):
        line_ref[pl.ds(pl.multiple_of(SUB + t * rows, SUB), rows)] = x

    receive_all(0, to_line)

    def filtered(start):
        window = line_ref[pl.ds(pl.multiple_of(start, SUB), SUB + step)]
        total = taps[0:1] * window[SUB:]
        for p in range(1, taps.shape[0]):
            total = total + taps[p : p + 1] * window[SUB - p : SUB - p + step]
        return total

    def starts_of(pair):
        return [pl.multiple_of((2 * pair + i) * step, step) for i in range(2)]

    def outer_in(pair, carry):
        starts = starts_of(pair)
        tall = [jnp.concatenate([filtered(a * length + start) for a in range(radix)], axis=0) for start in starts]
        for start, y in zip(starts, left(outer_m, tall, False)):
            part = pl.ds(start, step)
            u_ref[:, part, :] = turned(y.reshape(radix, step, LANES), (t1_re[:, part, :], t1_im[:, part, :]))
        return carry

    lax.fori_loop(0, radix // 2, outer_in, 0)

    def inner_in(pair, carry):
        for i, y in enumerate(left(inner_m, [u_ref[2 * pair], u_ref[2 * pair + 1]], False)):
            z_ref[2 * pair + i] = turned(y, (t2_re[2 * pair + i], t2_im[2 * pair + i]))
        return carry

    lax.fori_loop(0, radix // 2, inner_in, 0)

    def bins_of(t):
        return pl.ds(pl.multiple_of(t * SUB, SUB), SUB)

    send_all(1, lambda t: z_ref[:, bins_of(t), :].reshape(rows, LANES), 1.0)

    def row_in(t, x):
        x_ref[t] = turned(right(minus_m, x), (twist_re[t], twist_im[t]), True)

    receive_all(1, row_in)

    def half_copy(trip, c):
        part = pl.ds(pl.multiple_of(2 * c * SUB, 2 * SUB), 2 * SUB)
        return pltpu.make_async_remote_copy(
            src_ref=mine_ref.at[trip, :, part, :],
            dst_ref=theirs_ref.at[trip, :, part, :],
            send_sem=half_sent.at[trip, c],
            recv_sem=half_arrived.at[trip, c],
            device_id={"sub": 1 - parity},
            device_id_type=MESH,
        )

    def rows_forward(c, carry):
        parts = pair_of(c)
        for part, y in zip(parts, across(c, [x_ref[:, part, :] for part in parts], False)):
            mine_ref[0, :, part, :] = turned(y, (turn_re[...], turn_im[...]), True)
        half_copy(0, c).start()
        return carry

    lax.fori_loop(0, chunks, rows_forward, 0)

    def respond(c, carry):
        half_copy(0, c).wait_recv()
        for part in pair_of(c):
            both = theirs_ref[0, :, part, :] + sign * mine_ref[0, :, part, :]
            mine_ref[1, :, part, :] = turned(both, (resp_re[:, part, :], resp_im[:, part, :]))
        half_copy(1, c).start()
        return carry

    lax.fori_loop(0, chunks, respond, 0)

    def rows_back(c, carry):
        half_copy(1, c).wait_recv()
        parts = pair_of(c)
        both = [theirs_ref[1, :, part, :] + sign * mine_ref[1, :, part, :] for part in parts]
        for part, y in zip(parts, across(c, [turned(x, (turn_re[...], turn_im[...])) for x in both], True)):
            v_ref[:, part, :] = y
        return carry

    lax.fori_loop(0, chunks, rows_back, 0)
    send_all(2, row_out, 1.0)

    def to_bins(t, x):
        z_ref[:, bins_of(t), :] = x.reshape(radix, SUB, LANES)

    receive_all(2, to_bins)

    def inner_out(pair, carry):
        qs = (2 * pair, 2 * pair + 1)
        for q, y in zip(qs, left(inner_m, [turned(z_ref[q], (t2_re[q], t2_im[q]), True) for q in qs], True)):
            u_ref[q] = turned(y, (t1_re[q], t1_im[q]), True)
        return carry

    lax.fori_loop(0, radix // 2, inner_out, 0)

    def outer_out(pair, carry):
        starts = starts_of(pair)
        got_back = left(outer_m, [u_ref[:, pl.ds(start, step), :].reshape(length, LANES) for start in starts], True)
        for start, y in zip(starts, got_back):
            for a in range(radix):
                line_ref[pl.ds(pl.multiple_of(a * length + start, step), step)] = y[a * step : (a + 1) * step]
        return carry

    lax.fori_loop(0, radix // 2, outer_out, 0)
    send_all(3, lambda t: line_ref[pl.ds(pl.multiple_of(t * rows, SUB), rows)], norm_out)

    def to_out(t, x):
        out_ref[t] = x

    receive_all(3, to_out)

    def finish(i, carry):
        peer = lax.rem(me + route(i, n), n)
        for phase in range(4):
            for copy in copies(phase, i, peer, me):
                copy.wait_send()
        return carry

    lax.fori_loop(0, n - 1, finish, 0)

    def finish_halves(c, carry):
        for trip in range(2):
            half_copy(trip, c).wait_send()
        return carry

    lax.fori_loop(0, chunks, finish_halves, 0)


def as_parts(matrix):
    hi = matrix.astype(bf16)
    lo = (matrix - hi.astype(np.float64)).astype(bf16)
    return jnp.asarray(hi), jnp.asarray(lo)


def roots(left_count, right_count, length, direction):
    product = np.arange(left_count)[:, None] * np.arange(right_count)[None, :] % length
    return np.exp(direction * 2j * np.pi * product / length)


def left_parts(length, copies):
    full = np.kron(roots(length, length, length, -1), np.eye(copies))
    return as_parts(np.concatenate([full.real, full.imag], axis=1))


def right_parts(length, direction):
    full = roots(length, length, length, direction)
    return as_parts(np.block([[full.real, full.imag], [-full.imag, full.real]]))


def lane_table(values):
    re, im = values.real, values.imag
    return (
        jnp.asarray(np.concatenate([re, re], axis=-1), f32),
        jnp.asarray(np.concatenate([-im, im], axis=-1), f32),
    )


def body(channels, synth_taps, chirp_phase):
    frames_dev, half = channels.shape[1:]
    n = lax.axis_size("tm")
    me = lax.axis_index("tm")
    parity = lax.axis_index("sub")
    frames = frames_dev * n
    series_len = frames * 2 * half
    radix, length = SUB, frames // SUB
    tap_count = synth_taps.shape[0]

    def partner(x):
        size = lax.axis_size("sub")
        return lax.ppermute(x, "sub", [(i, size - 1 - i) for i in range(size)])

    long_m = left_parts(n, SUB)
    outer_m = left_parts(radix, length // radix)
    inner_m = left_parts(length, 1)
    short_plus, short_minus = right_parts(WIDTH, 1), right_parts(WIDTH, -1)

    twist = lane_table(roots(n, WIDTH, half, 1)[:, None, :])
    turn = np.exp(1j * np.pi * np.arange(half) / half).reshape(n, 1, WIDTH)
    turns = lane_table(np.stack([np.ones_like(turn), turn]))
    taps = lax.dynamic_index_in_dim(synth_taps.reshape(tap_count, WIDTH, n), me, 2, keepdims=False)
    taps = jnp.concatenate([taps, taps], axis=-1)
    args = (
        channels, partner(channels), taps, chirp_phase, *turns, *twist, *long_m, *inner_m, *outer_m, *short_plus,
        *short_minus,
    )
    grid_shape, tower = (n, frames_dev, LANES), (radix, length, LANES)
    phases = 4
    out = pl.pallas_call(
        functools.partial(beam_kernel, 1.0 / math.sqrt(2 * half), 1.0 / series_len),
        out_shape=jax.ShapeDtypeStruct(grid_shape, f32),
        in_specs=[pl.BlockSpec(memory_space=pltpu.VMEM)] * len(args),
        out_specs=pl.BlockSpec(memory_space=pltpu.VMEM),
        scratch_shapes=[
            pltpu.VMEM(grid_shape, f32),
            pltpu.VMEM(grid_shape, f32),
            pltpu.VMEM(tower, f32),
            pltpu.VMEM(tower, f32),
            pltpu.VMEM((SUB + frames, LANES), f32),
            *[pltpu.VMEM(tower, f32)] * 4,
            *[pltpu.VMEM(grid_shape, f32)] * 2,
            pltpu.VMEM((2, *grid_shape), f32),
            pltpu.VMEM((2, *grid_shape), f32),
            pltpu.VMEM((phases, *grid_shape), bf16),
            pltpu.VMEM((phases, n, 1, LANES), f32),
            pltpu.VMEM((phases, *grid_shape), bf16),
            pltpu.VMEM((phases, n, 1, LANES), f32),
            *[pltpu.SemaphoreType.DMA((phases, n))] * 4,
            *[pltpu.SemaphoreType.DMA((2, frames_dev // (2 * SUB)))] * 2,
        ],
        compiler_params=pltpu.CompilerParams(collective_id=1, has_side_effects=True, vmem_limit_bytes=56 * 2**20),
        name="beam",
    )(*args)
    out = out.reshape(n, frames_dev, 2, WIDTH).transpose(2, 1, 3, 0)
    return out.reshape(2, frames_dev, 1, half)


def solution(mesh):
    placed = (P(None, ("beam", "tm"), "sub"), P(None, "sub", None), P("tm", "sub"))
    return jax.shard_map(
        body,
        mesh=mesh,
        in_specs=placed,
        out_specs=P(None, ("beam", "tm"), "sub", None),
        check_vma=False,
    )
```

time: 751 us -> 262 us (0.35); the launches traced: 740 us -> 262 us
  waiting for transfers between devices: 469 us -> 0.31 us
  Pallas kernels: 0 us -> 254 us
  matrix products: 104 us -> 0 us
  starting transfers between devices: 78.6 us -> 0.01 us
  local copies, waits for them, and re-layouts: 50.5 us -> 6.23 us
  other arithmetic: 36.8 us -> 1.51 us
    all_to_all x8 -> x0, waiting for transfers between devices: 465 us -> none  [the longest x2 125 us: to_columns(): lax.all_to_all(re_part.T, 'tm', split_axis=0, concat_axis=1, tiled=True)]
    pallas_call x0 -> x1, Pallas kernels: none -> 254 us  [body(): pl.pallas_call(functools.partial(beam_kernel, 1.0 / math.sqrt(2 * half),...]
    dot_general x40 -> x0, matrix products: 104 us -> none  [contract(): return jnp.einsum(form, former, latter, precision=highest)]
    all_to_all x8 -> x0, starting transfers between devices: 68.4 us -> none  [the longest x2 38 us: to_columns(): lax.all_to_all(re_part.T, 'tm', split_axis=0, concat_axis=1, tiled=True)]
    add x8 -> x0, other arithmetic: 19 us -> none  [the longest x5 10.4 us: complex_times(): left_re * right_im + left_im * right_re]
    unnamed x36 -> x2, local copies, waits for them, and re-layouts: 19.3 us -> 0.79 us
    all_to_all x8 -> x0, other arithmetic: 16.3 us -> none  [the longest x2 5.45 us: to_columns(): lax.all_to_all(im_part.T, 'tm', split_axis=0, concat_axis=1, tiled=True)]
    ppermute x8 -> x1, starting transfers between devices: 10.2 us -> 0.01 us  [partner(): return lax.ppermute(x, 'sub', [(i, size - 1 - i) for i in range(size)])]
  transfers between devices with their start and end apart: 16 -> 1, of which waited for: 13 -> 1; matrix products, arithmetic and copies ran while one was open for 6% -> 1% of each run, Pallas kernels for 0% -> 0%
where the time goes in v1:
time: 262 us
  Pallas kernels  254 us (97%)
  local copies, waits for them, and re-layouts  6.23 us (2%)
    pallas_call x1, Pallas kernels, body(): pl.pallas_call(functools.partial(beam_kernel, 1.0 / math.sqrt(2 * half),...  254 us
  transfers between devices with their start and end apart: 1, of which 1 were waited for; matrix products, arithmetic and copies ran while one was open for 1% of the time, Pallas kernels for 0%

profile of v1, /device:TPU:46, one launch (start us, length us, event | category | flops | bytes accessed | tf_op | source)
XLA Modules:
  0.0 262.1 jit_solution(14570267237941886919)
XLA Ops:
  0.0 0.0 collective-permute-start
  0.0 0.8 reduce
  0.8 0.1 reshape.9
  0.9 0.2 dynamic-slice_reduce_fusion
  1.1 0.7 pad_maximum_fusion.taps
  1.8 0.3 collective-permute-done.other
  2.1 0.0 copy-start
  2.1 0.8 copy-done
  2.9 254.0 %beam.1 = f32[32,64,128]{2,1,0:T(8,128)} custom-call(bf16[2,64,2048]{2,1,0:T(8,128)(2,1)} %own.1, bf16[2,64,2048]{2,1,0:T(8,128)(2,1)} %copy-done, f32[4,128]{1,0:T(4,128)} %pad_maximum_fusion.taps, f32[64,2048]{1,0:T(8,128)} %phase_ref.1, f32[2,32,1,128]{3,2,1,0:T(1,128)} %constant.52.clone.turns_re, f32[2,32,1,128]{3,2,1,0:T(1,128)} %constant.53.clone.turns_im, ...), custom_call_target="tpu_custom_call" | custom-call | tf_op jit(solution)/shard_map/beam/pallas_call | solution.py:407
  256.9 3.1 %copy.24 = f32[32,64,128]{1,0,2:T(8,128)S(1)} copy(f32[32,64,128]{2,1,0:T(8,128)} %beam.1) | data formatting | bytes 2097152 | tf_op jit(solution)/shard_map/reshape | solution.py:432
  260.0 2.1 copy.23
Async XLA Ops:
  0.0 2.1 collective-permute-start
  2.1 0.8 copy-start

commit v2 on v1

--- a/solution.py
+++ b/solution.py
@@ -16,6 +16,7 @@
 WIDTH = 64
 LANES = 2 * WIDTH
 SUB = 8
+GROUPS = 4
 
 SPAN = 160.0
 BASE = SPAN / 2
@@ -90,6 +91,11 @@
 
 def route(i, n):
     return n // 2 + (i + 1) // 2 * (2 * lax.rem(i, 2) - 1)
+
+
+def group_route(group, i, n):
+    count = n // GROUPS
+    return group + GROUPS * lax.rem(count // 2 + (i + 1) // 2 * (1 - 2 * lax.rem(i, 2)) + count, count)
 
 
 def beam_kernel(norm_in, norm_out, own, other, taps, phase_ref, turns_re, turns_im, twist_re, twist_im, long_hi, long_lo,
@@ -117,44 +123,66 @@
     lax.fori_loop(0, n - 1, greet, 0)
     pl.semaphore_signal(barrier, inc=1, device_id={"sub": 1 - parity}, device_id_type=MESH)
 
-    def copies(phase, i, peer, slot):
-        pairs = ((put_scale, got_scale, sent_scale, arrived_scale), (put, got, sent, arrived))
+    def copies(trip, d, count):
+        peer = lax.rem(me + d, n)
+        part = pl.ds(0, count)
+        kinds = (
+            (put_scale.at[trip, peer], got_scale.at[trip, me], sent_scale, arrived_scale),
+            (put.at[trip, peer, part, :], got.at[trip, me, part, :], sent, arrived),
+        )
         return [
             pltpu.make_async_remote_copy(
-                src_ref=source.at[phase, peer],
-                dst_ref=target.at[phase, slot],
-                send_sem=out_sem.at[phase, i],
-                recv_sem=in_sem.at[phase, i],
+                src_ref=source,
+                dst_ref=target,
+                send_sem=out_sem.at[trip, d],
+                recv_sem=in_sem.at[trip, d],
                 device_id={"tm": peer},
                 device_id_type=MESH,
             )
-            for source, target, out_sem, in_sem in pairs
+            for source, target, out_sem, in_sem in kinds
         ]
 
-    def send_all(phase, held, norm):
-
-        def send(i, carry):
-            peer = lax.rem(me + route(i, n), n)
-            put[phase, peer], put_scale[phase, peer] = encode(held(peer), norm)
-            for copy in copies(phase, i, peer, me):
-                copy.start()
+    def keep(trip, count, held, norm):
+        got[trip, me, 0:count, :], got_scale[trip, me] = encode(held(me), norm)
+
+    def send(trip, count, d, held, norm):
+        peer = lax.rem(me + d, n)
+        put[trip, peer, 0:count, :], put_scale[trip, peer] = encode(held(peer), norm)
+        for copy in copies(trip, d, count):
+            copy.start()
+
+    def take(trip, count, d, use):
+        source = lax.rem(me + n - d, n)
+        for copy in copies(trip, d, count):
+            copy.wait_recv()
+        use(source, decode(got[trip, source, 0:count, :], got_scale[trip, source]))
+
+    def take_own(trip, count, use):
+        use(me, decode(got[trip, me, 0:count, :], got_scale[trip, me]))
+
+    def each(count, act):
+
+        def step_of(i, carry):
+            act(i)
             return carry
 
-        lax.fori_loop(0, n - 1, send, 0)
-        got[phase, me], got_scale[phase, me] = encode(held(me), norm)
-
-    def receive_all(phase, use):
-        use(me, decode(got[phase, me], got_scale[phase, me]))
-
-        def receive(i, carry):
-            d = route(i, n)
-            source = lax.rem(me + n - d, n)
-            for copy in copies(phase, i, lax.rem(me + d, n), source):
-                copy.wait_recv()
-            use(source, decode(got[phase, source], got_scale[phase, source]))
-            return carry
-
-        lax.fori_loop(0, n - 1, receive, 0)
+        lax.fori_loop(0, count, step_of, 0)
+
+    def send_all(trip, count, held, norm):
+        each(n - 1, lambda i: send(trip, count, route(i, n), held, norm))
+        keep(trip, count, held, norm)
+
+    def take_all(trip, count, use):
+        take_own(trip, count, use)
+        each(n - 1, lambda i: take(trip, count, route(i, n), use))
+
+    group_size = n // GROUPS
+
+    def send_group(trip, group, held, norm):
+        each(group_size - (group == 0), lambda i: send(trip, rows, group_route(group, i, n), held, norm))
+
+    def take_group(trip, group, use):
+        each(group_size - (group == 0), lambda i: take(trip, rows, group_route(group, i, n), use))
 
     def pair_of(c):
         return [pl.ds(pl.multiple_of((2 * c + i) * SUB, SUB), SUB) for i in range(2)]
@@ -162,8 +190,8 @@
     def across(c, blocks, conj):
         return [y.reshape(n, SUB, LANES) for y in left(long_m, [x.reshape(n * SUB, LANES) for x in blocks], conj)]
 
-    def row_out(t):
-        return right(plus_m, turned(v_ref[t], (twist_re[t], twist_im[t])))
+    def row_out(t, part=slice(None)):
+        return right(plus_m, turned(v_ref[t, part, :], (twist_re[t], twist_im[t])))
 
     low = lax.broadcasted_iota(jnp.int32, (1, LANES), 1) < WIDTH
     for j in range(n // 2):
@@ -183,7 +211,9 @@
 
     lax.fori_loop(0, chunks, first_rows, 0)
     pl.semaphore_wait(barrier, n)
-    send_all(0, row_out, norm_in)
+    for group in range(GROUPS):
+        send_group(0, group, row_out, norm_in)
+    keep(0, rows, row_out, norm_in)
 
     lane = lax.broadcasted_iota(jnp.int32, (1, LANES), 1)
     row = lax.broadcasted_iota(jnp.int32, (length, 1), 0)
@@ -219,8 +249,6 @@
     def to_line(t, x):
         line_ref[pl.ds(pl.multiple_of(SUB + t * rows, SUB), rows)] = x
 
-    receive_all(0, to_line)
-
     def filtered(start):
         window = line_ref[pl.ds(pl.multiple_of(start, SUB), SUB + step)]
         total = taps[0:1] * window[SUB:]
@@ -239,24 +267,26 @@
             u_ref[:, part, :] = turned(y.reshape(radix, step, LANES), (t1_re[:, part, :], t1_im[:, part, :]))
         return carry
 
-    lax.fori_loop(0, radix // 2, outer_in, 0)
+    take_own(0, rows, to_line)
+    for group in range(GROUPS):
+        take_group(0, group, to_line)
+        if group:
+            outer_in(lax.rem(me + n - group + 1, GROUPS), 0)
+    outer_in(lax.rem(me + n - GROUPS + 1, GROUPS), 0)
 
     def inner_in(pair, carry):
         for i, y in enumerate(left(inner_m, [u_ref[2 * pair], u_ref[2 * pair + 1]], False)):
             z_ref[2 * pair + i] = turned(y, (t2_re[2 * pair + i], t2_im[2 * pair + i]))
         return carry
 
-    lax.fori_loop(0, radix // 2, inner_in, 0)
-
     def bins_of(t):
         return pl.ds(pl.multiple_of(t * SUB, SUB), SUB)
 
-    send_all(1, lambda t: z_ref[:, bins_of(t), :].reshape(rows, LANES), 1.0)
-
-    def row_in(t, x):
-        x_ref[t] = turned(right(minus_m, x), (twist_re[t], twist_im[t]), True)
-
-    receive_all(1, row_in)
+    half_rows, half_radix = rows // 2, radix // 2
+    for h in range(2):
+        lax.fori_loop(h * half_radix // 2, (h + 1) * half_radix // 2, inner_in, 0)
+        towers = slice(h * half_radix, (h + 1) * half_radix)
+        send_all(1 + h, half_rows, lambda t: z_ref[towers, bins_of(t), :].reshape(half_rows, LANES), 1.0)
 
     def half_copy(trip, c):
         part = pl.ds(pl.multiple_of(2 * c * SUB, 2 * SUB), 2 * SUB)
@@ -276,8 +306,6 @@
         half_copy(0, c).start()
         return carry
 
-    lax.fori_loop(0, chunks, rows_forward, 0)
-
     def respond(c, carry):
         half_copy(0, c).wait_recv()
         for part in pair_of(c):
@@ -286,8 +314,6 @@
         half_copy(1, c).start()
         return carry
 
-    lax.fori_loop(0, chunks, respond, 0)
-
     def rows_back(c, carry):
         half_copy(1, c).wait_recv()
         parts = pair_of(c)
@@ -296,13 +322,16 @@
             v_ref[:, part, :] = y
         return carry
 
-    lax.fori_loop(0, chunks, rows_back, 0)
-    send_all(2, row_out, 1.0)
-
-    def to_bins(t, x):
-        z_ref[:, bins_of(t), :] = x.reshape(radix, SUB, LANES)
-
-    receive_all(2, to_bins)
+    for h in range(2):
+        part = slice(h * half_rows, (h + 1) * half_rows)
+
+        def row_in(t, x):
+            x_ref[t, part, :] = turned(right(minus_m, x), (twist_re[t], twist_im[t]), True)
+
+        take_all(1 + h, half_rows, row_in)
+        for act in (rows_forward, respond, rows_back):
+            lax.fori_loop(h * chunks // 2, (h + 1) * chunks // 2, act, 0)
+        send_all(3 + h, half_rows, lambda t: row_out(t, part), 1.0)
 
     def inner_out(pair, carry):
         qs = (2 * pair, 2 * pair + 1)
@@ -310,7 +339,14 @@
             u_ref[q] = turned(y, (t1_re[q], t1_im[q]), True)
         return carry
 
-    lax.fori_loop(0, radix // 2, inner_out, 0)
+    for h in range(2):
+        towers = slice(h * half_radix, (h + 1) * half_radix)
+
+        def to_bins(t, x):
+            z_ref[towers, bins_of(t), :] = x.reshape(half_radix, SUB, LANES)
+
+        take_all(3 + h, half_rows, to_bins)
+        lax.fori_loop(h * half_radix // 2, (h + 1) * half_radix // 2, inner_out, 0)
 
     def outer_out(pair, carry):
         starts = starts_of(pair)
@@ -320,22 +356,27 @@
                 line_ref[pl.ds(pl.multiple_of(a * length + start, step), step)] = y[a * step : (a + 1) * step]
         return carry
 
-    lax.fori_loop(0, radix // 2, outer_out, 0)
-    send_all(3, lambda t: line_ref[pl.ds(pl.multiple_of(t * rows, SUB), rows)], norm_out)
+    def frames_of(t):
+        return line_ref[pl.ds(pl.multiple_of(t * rows, SUB), rows)]
+
+    for group in range(GROUPS):
+        outer_out(lax.rem(me + group, GROUPS), 0)
+        send_group(5, group, frames_of, norm_out)
+    keep(5, rows, frames_of, norm_out)
 
     def to_out(t, x):
         out_ref[t] = x
 
-    receive_all(3, to_out)
-
-    def finish(i, carry):
-        peer = lax.rem(me + route(i, n), n)
-        for phase in range(4):
-            for copy in copies(phase, i, peer, me):
+    take_own(5, rows, to_out)
+    for group in range(GROUPS):
+        take_group(5, group, to_out)
+
+    def finish(i):
+        for trip, count in enumerate((rows, *[half_rows] * 4, rows)):
+            for copy in copies(trip, i + 1, count):
                 copy.wait_send()
-        return carry
-
-    lax.fori_loop(0, n - 1, finish, 0)
+
+    each(n - 1, finish)
 
     def finish_halves(c, carry):
         for trip in range(2):
@@ -403,7 +444,7 @@
         *short_minus,
     )
     grid_shape, tower = (n, frames_dev, LANES), (radix, length, LANES)
-    phases = 4
+    trips = 6
     out = pl.pallas_call(
         functools.partial(beam_kernel, 1.0 / math.sqrt(2 * half), 1.0 / series_len),
         out_shape=jax.ShapeDtypeStruct(grid_shape, f32),
@@ -419,11 +460,11 @@
             *[pltpu.VMEM(grid_shape, f32)] * 2,
             pltpu.VMEM((2, *grid_shape), f32),
             pltpu.VMEM((2, *grid_shape), f32),
-            pltpu.VMEM((phases, *grid_shape), bf16),
-            pltpu.VMEM((phases, n, 1, LANES), f32),
-            pltpu.VMEM((phases, *grid_shape), bf16),
-            pltpu.VMEM((phases, n, 1, LANES), f32),
-            *[pltpu.SemaphoreType.DMA((phases, n))] * 4,
+            pltpu.VMEM((trips, *grid_shape), bf16),
+            pltpu.VMEM((trips, n, 1, LANES), f32),
+            pltpu.VMEM((trips, *grid_shape), bf16),
+            pltpu.VMEM((trips, n, 1, LANES), f32),
+            *[pltpu.SemaphoreType.DMA((trips, n))] * 4,
             *[pltpu.SemaphoreType.DMA((2, frames_dev // (2 * SUB)))] * 2,
         ],
         compiler_params=pltpu.CompilerParams(collective_id=1, has_side_effects=True, vmem_limit_bytes=56 * 2**20),

time: 262 us -> 255 us (0.973)
  Pallas kernels: 254 us -> 247 us
    pallas_call x1, Pallas kernels: 254 us -> 247 us  [body(): pl.pallas_call(functools.partial(beam_kernel, 1.0 / math.sqrt(2 * half),...]
where the time goes in v2:
time: 255 us
  Pallas kernels  247 us (97%)
  local copies, waits for them, and re-layouts  6.23 us (2%)
    pallas_call x1, Pallas kernels, body(): pl.pallas_call(functools.partial(beam_kernel, 1.0 / math.sqrt(2 * half),...  247 us
  transfers between devices with their start and end apart: 1, of which 1 were waited for; matrix products, arithmetic and copies ran while one was open for 1% of the time, Pallas kernels for 0%

profile of v2, /device:TPU:46, one launch (start us, length us, event | category | flops | bytes accessed | tf_op | source)
XLA Modules:
  0.0 254.9 jit_solution(18020074730960737270)
XLA Ops:
  0.0 0.0 collective-permute-start
  0.0 0.8 reduce
  0.8 0.1 reshape.9
  0.9 0.2 dynamic-slice_reduce_fusion
  1.1 0.7 pad_maximum_fusion.taps
  1.8 0.3 collective-permute-done.other
  2.1 0.0 copy-start
  2.1 0.8 copy-done
  2.9 246.8 %beam.1 = f32[32,64,128]{2,1,0:T(8,128)} custom-call(bf16[2,64,2048]{2,1,0:T(8,128)(2,1)} %own.1, bf16[2,64,2048]{2,1,0:T(8,128)(2,1)} %copy-done, f32[4,128]{1,0:T(4,128)} %pad_maximum_fusion.taps, f32[64,2048]{1,0:T(8,128)} %phase_ref.1, f32[2,32,1,128]{3,2,1,0:T(1,128)} %constant.52.clone.turns_re, f32[2,32,1,128]{3,2,1,0:T(1,128)} %constant.53.clone.turns_im, ...), custom_call_target="tpu_custom_call" | custom-call | tf_op jit(solution)/shard_map/beam/pallas_call | solution.py:448
  249.7 3.1 %copy.24 = f32[32,64,128]{1,0,2:T(8,128)S(1)} copy(f32[32,64,128]{2,1,0:T(8,128)} %beam.1) | data formatting | bytes 2097152 | tf_op jit(solution)/shard_map/reshape | solution.py:473
  252.8 2.1 copy.23
Async XLA Ops:
  0.0 2.1 collective-permute-start
  2.1 0.8 copy-start

commit v3 on v2

--- a/solution.py
+++ b/solution.py
@@ -90,7 +90,9 @@
 
 
 def route(i, n):
-    return n // 2 + (i + 1) // 2 * (2 * lax.rem(i, 2) - 1)
+    turn, near = lax.rem(i + 3, 4), (i + 3) // 4
+    far, back = turn // 2, lax.rem(turn, 2)
+    return far * (n // 2) + (1 - far) * back * n + (1 - 2 * back) * (1 - 2 * far) * near
 
 
 def group_route(group, i, n):
@@ -365,7 +367,7 @@
     keep(5, rows, frames_of, norm_out)
 
     def to_out(t, x):
-        out_ref[t] = x
+        out_ref[:, pl.ds(t, 1), :] = x.T[:, None, :]
 
     take_own(5, rows, to_out)
     for group in range(GROUPS):
@@ -447,7 +449,7 @@
     trips = 6
     out = pl.pallas_call(
         functools.partial(beam_kernel, 1.0 / math.sqrt(2 * half), 1.0 / series_len),
-        out_shape=jax.ShapeDtypeStruct(grid_shape, f32),
+        out_shape=jax.ShapeDtypeStruct((LANES, n, frames_dev), f32),
         in_specs=[pl.BlockSpec(memory_space=pltpu.VMEM)] * len(args),
         out_specs=pl.BlockSpec(memory_space=pltpu.VMEM),
         scratch_shapes=[
@@ -470,7 +472,7 @@
         compiler_params=pltpu.CompilerParams(collective_id=1, has_side_effects=True, vmem_limit_bytes=56 * 2**20),
         name="beam",
     )(*args)
-    out = out.reshape(n, frames_dev, 2, WIDTH).transpose(2, 1, 3, 0)
+    out = out.reshape(2, half, frames_dev).transpose(0, 2, 1)
     return out.reshape(2, frames_dev, 1, half)
 
 

time: 255 us -> 253 us (level)
  no operation moved by 1% of the time
where the time goes in v3:
time: 253 us
  Pallas kernels  246 us (97%)
  local copies, waits for them, and re-layouts  4.94 us (2%)
    pallas_call x1, Pallas kernels, body(): pl.pallas_call(functools.partial(beam_kernel, 1.0 / math.sqrt(2 * half),...  246 us
  transfers between devices with their start and end apart: 1, of which 1 were waited for; matrix products, arithmetic and copies ran while one was open for 1% of the time, Pallas kernels for 0%

profile of v3, /device:TPU:46, one launch (start us, length us, event | category | flops | bytes accessed | tf_op | source)
XLA Modules:
  0.0 253.1 jit_solution(1385634895856618236)
XLA Ops:
  0.0 0.0 collective-permute-start
  0.0 0.8 reduce
  0.8 0.1 reshape.9
  0.9 0.2 dynamic-slice_reduce_fusion
  1.1 0.7 pad_maximum_fusion.taps
  1.8 0.3 collective-permute-done.other
  2.1 0.0 copy-start
  2.1 0.8 copy-done
  2.9 246.3 %beam.1 = f32[128,32,64]{2,1,0:T(8,128)} custom-call(bf16[2,64,2048]{2,1,0:T(8,128)(2,1)} %own.1, bf16[2,64,2048]{2,1,0:T(8,128)(2,1)} %copy-done, f32[4,128]{1,0:T(4,128)} %pad_maximum_fusion.taps, f32[64,2048]{1,0:T(8,128)} %phase_ref.1, f32[2,32,1,128]{3,2,1,0:T(1,128)} %constant.52.clone.turns_re, f32[2,32,1,128]{3,2,1,0:T(1,128)} %constant.53.clone.turns_im, ...), custom_call_target="tpu_custom_call" | custom-call | tf_op jit(solution)/shard_map/beam/pallas_call | solution.py:450
  249.2 2.2 copy.21
  251.4 1.7 reshape.11
Async XLA Ops:
  0.0 2.1 collective-permute-start
  2.1 0.8 copy-start
